TPU v7x, 256 devices: a whole 4x4x8 slice. The times are simulated.
256 devices in a mesh: pt: 8 (over x, y_lo), tp: 32 (over y_hi, z, core).
Axes of the slice: x: 4, y: 4 (y_hi: 2, y_lo: 2; y = y_hi * 2 + y_lo), z: 8, core: 2. Of those that a mesh axis runs over, the one named last changes fastest.
Arguments:
- tokens: bfloat16 [4096, 4096], P('pt', 'tp'), may hold values from -6 to 6
- t_values: float32 [8], replicated, may hold values from 0.05 to 0.95
- gate_start: bfloat16 [4096, 14336], P('pt', 'tp'), may hold values from -0.09375 to 0.09375
- gate_bend: bfloat16 [4096, 14336], P('pt', 'tp'), may hold values from -0.1875 to 0.1875
- gate_end: bfloat16 [4096, 14336], P('pt', 'tp'), may hold values from -0.09375 to 0.09375
- up_start: bfloat16 [4096, 14336], P('pt', 'tp'), may hold values from -0.09375 to 0.09375
- up_bend: bfloat16 [4096, 14336], P('pt', 'tp'), may hold values from -0.1875 to 0.1875
- up_end: bfloat16 [4096, 14336], P('pt', 'tp'), may hold values from -0.09375 to 0.09375
- hidden_grad: bfloat16 [4096, 14336], P('pt', 'tp'), may hold values from -6 to 6
Outputs:
- hidden: bfloat16 [4096, 14336], P('pt', 'tp')
- input_grad: bfloat16 [4096, 4096], P('pt', 'tp')
- gate_bend_grad: float32 [4096, 14336], P('pt', 'tp')
- up_bend_grad: float32 [4096, 14336], P('pt', 'tp')
All inputs are finite; a program needn't handle non-finite values.
Results may differ from a plain program's by a relative error of at most 0.014.
Values may be sent and summed in bfloat16 or wider, within the bound.
A program may use at most 128 MiB of HBM per device.

v0:
```python
import jax
import jax.numpy as jnp
from jax import lax
from jax.sharding import PartitionSpec as P


def in_one_piece(arrays, axis, split_dim, concat_dim, along):
    both = jnp.concatenate(arrays, axis=along)
    filled, at, finished = (
        lax.all_to_all(both, axis, split_axis=split_dim, concat_axis=concat_dim, tiled=True),
        0,
        [],
    )
    for a in arrays:
        finished.append(lax.slice_in_dim(filled, at, at + a.shape[along], axis=along))
        at += a.shape[along]
    return tuple(finished)


def cut_along(array, dim, size):
    before, after = (array.shape[:dim], array.shape[dim + 1 :])
    return jnp.moveaxis(array.reshape(*before, size, -1, *after), dim, 0)


def summed_on_arrival(array, axis, dim):
    parts = cut_along(array, dim, lax.axis_size(axis))
    arrived = lax.all_to_all(parts, axis, split_axis=0, concat_axis=0, tiled=True)
    return arrived.astype(jnp.float32).sum(axis=0)


def in_one_piece_2(arrays, axis, dim, along):
    ends, at = ([], 0)
    for a in arrays[:-1]:
        at += a.shape[along]
        ends.append(at)
    both = jnp.concatenate(arrays, axis=along)
    return tuple(
        jnp.split(lax.psum_scatter(both, axis, scatter_dimension=dim, tiled=True), ends, axis=along)
    )


def blend_all(first, middle, last, start, bend, end):
    mixed = (
        first[:, None, None] * start.astype(jnp.float32)[None]
        + middle[:, None, None] * bend.astype(jnp.float32)[None]
        + last[:, None, None] * end.astype(jnp.float32)[None]
    )
    return mixed.astype(jnp.bfloat16)


def per_device(
    tokens, t_values, gate_start, gate_bend, gate_end, up_start, up_bend, up_end, hidden_grad
):
    mine = lax.axis_index("pt")
    first = (1.0 - t_values) ** 2
    middle = 2.0 * t_values * (1.0 - t_values)
    last = t_values * t_values
    gate_parts = blend_all(first, middle, last, gate_start, gate_bend, gate_end)
    up_parts = blend_all(first, middle, last, up_start, up_bend, up_end)
    gate_full, up_full = in_one_piece((gate_parts, up_parts), "pt", 0, 1, 2)
    gate_w = gate_full[0]
    up_w = up_full[0]
    whole = lax.all_gather(tokens, "tp", axis=1, tiled=True)
    gate = jnp.dot(whole, gate_w, preferred_element_type=jnp.float32)
    up = jnp.dot(whole, up_w, preferred_element_type=jnp.float32)
    sig = jax.nn.sigmoid(gate)
    act = gate * sig
    hidden = (act * up).astype(jnp.bfloat16)
    cotf = hidden_grad.astype(jnp.float32)
    d_up = cotf * act
    d_gate = cotf * up * sig * (1.0 + gate * (1.0 - sig))
    d_gate_b = d_gate.astype(jnp.bfloat16)
    d_up_b = d_up.astype(jnp.bfloat16)
    weight_here = lax.dynamic_index_in_dim(middle, mine, 0, keepdims=False)
    scaled_gate = (weight_here * d_gate).astype(jnp.bfloat16)
    scaled_up = (weight_here * d_up).astype(jnp.bfloat16)
    part_gate = lax.dot_general(
        gate_w, d_gate_b, (((1,), (1,)), ((), ())), preferred_element_type=jnp.float32
    )
    part_up = lax.dot_general(
        up_w, d_up_b, (((1,), (1,)), ((), ())), preferred_element_type=jnp.float32
    )
    input_cols = summed_on_arrival((part_gate + part_up).astype(jnp.bfloat16), "tp", 0)
    input_grad = input_cols.T.astype(jnp.bfloat16)
    full_gate = lax.dot_general(
        whole, scaled_gate, (((0,), (0,)), ((), ())), preferred_element_type=jnp.float32
    )
    full_up = lax.dot_general(
        whole, scaled_up, (((0,), (0,)), ((), ())), preferred_element_type=jnp.float32
    )
    gate_grad, up_grad = tuple(
        (
            part.astype(jnp.float32)
            for part in in_one_piece_2(
                (full_gate.astype(jnp.bfloat16), full_up.astype(jnp.bfloat16)), "pt", 0, 1
            )
        )
    )
    return (hidden, input_grad, gate_grad, up_grad)


def solution(mesh):
    return jax.shard_map(
        per_device,
        mesh=mesh,
        in_specs=(
            P("pt", "tp"),
            P(),
            P("pt", "tp"),
            P("pt", "tp"),
            P("pt", "tp"),
            P("pt", "tp"),
            P("pt", "tp"),
            P("pt", "tp"),
            P("pt", "tp"),
        ),
        out_specs=(P("pt", "tp"), P("pt", "tp"), P("pt", "tp"), P("pt", "tp")),
        check_vma=False,
    )
```

profile of v0, /device:TPU:1, one launch (start us, length us, event | category | flops | bytes accessed | tf_op | source)
XLA Modules:
  0.0 382.4 jit_solution(16434651966500397295)
XLA Ops:
  7.2 0.0 copy-start.1
  7.2 0.0 all-gather.2.cloned.1.call-start
  7.2 0.7 all-gather.2.cloned.1.call-update
  7.9 1.2 copy.19
  9.1 1.2 copy.20
  10.4 1.2 copy.21
  11.6 2.2 copy.22
  13.8 2.2 copy.23
  16.0 2.3 copy.24
  18.3 0.0 copy-done.1
  18.3 6.8 %add_convert_fusion.2 = (bf16[8,512,448]{2,1,0:T(8,128)(2,1)}, bf16[8,512,448]{2,1,0:T(8,128)(2,1)}) fusion(f32[512,448]{1,0:T(8,128)S(1)} %copy.21, f32[8]{0:T(128)S(1)} %get-tuple-element.13, f32[512,448]{1,0:T(8,128)S(1)} %copy.20, f32[8]{0:T(128)S(1)} %get-tuple-element.14, f32[512,448]{1,0:T(8,128)S(1)} %copy.19, f32[8]{0:T(128)S(1)} %get-tuple-element.12, ...), kind=kLoop, calls=%fused_computation.2 | loop fusion | flops 22020096 | bytes 12845152 | tf_op jit(solution)/shard_map/convert_element_type | solution.py:48
  25.1 9.4 %pad_maximum_fusion = bf16[8,512,896]{2,1,0:T(8,128)(2,1)} fusion(bf16[8,512,448]{2,1,0:T(8,128)(2,1)} %get-tuple-element.11, bf16[8,512,448]{2,1,0:T(8,128)(2,1)} %get-tuple-element.10), kind=kLoop, calls=%fused_computation.3 | loop fusion | flops 14680064 | bytes 14680064 | tf_op jit(solution)/shard_map/concatenate | solution.py:8
  34.5 5.8 %all-to-all-start = ((bf16[8,512,896]{2,1,0:T(8,128)(2,1)}), bf16[8,512,896]{2,1,0:T(8,128)(2,1)}, u32[]{:S(2)}, u32[]{:S(2)}) async-start(bf16[8,512,896]{2,1,0:T(8,128)(2,1)} %pad_maximum_fusion), calls=%async_computation | async-start | bytes 14680064 | tf_op jit(solution)/shard_map/all_to_all | solution.py:10
  40.3 0.2 reduce-scatter.2.cloned.1.call-start
  40.6 0.6 dynamic_slice.4
  41.2 99.8 %all-to-all-done = bf16[8,512,896]{2,1,0:T(8,128)(2,1)} async-done(((bf16[8,512,896]{2,1,0:T(8,128)(2,1)}), bf16[8,512,896]{2,1,0:T(8,128)(2,1)}, u32[]{:S(2)}, u32[]{:S(2)}) %all-to-all-start) | async-done | bytes 7340064 | tf_op jit(solution)/shard_map/all_to_all | solution.py:10
  141.0 11.6 %all-gather.2.cloned.1.call-done = bf16[512,4096]{1,0:T(8,128)(2,1)} async-done(((bf16[512,128]{1,0:T(8,128)(2,1)}), bf16[512,4096]{1,0:T(8,128)(2,1)}) %all-gather.2.cloned.1.call-update) | async-done | bytes 4194320 | tf_op jit(solution)/shard_map/all_gather | solution.py:63
  152.6 0.0 copy-start.2
  152.6 6.1 %fusion.6 = f32[512,448]{0,1:T(8,128)S(1)} fusion(bf16[512,4096]{1,0:T(8,128)(2,1)} %all-gather.2.cloned.1.call-done, bf16[1,4096,896]{2,1,0:T(8,128)(2,1)} %bitcast), kind=kOutput, calls=%fused_computation.15 | convolution fusion | flops 1879048192 | bytes 9306112 | tf_op jit(solution)/shard_map/dot_general | solution.py:64
  158.7 0.0 copy-done.2
  158.7 0.0 copy-start
  158.8 6.7 %multiply_convert_fusion.2 = (bf16[512,448]{0,1:T(8,128)(2,1)}, f32[512,448]{0,1:T(8,128)S(1)}) fusion(f32[512,448]{0,1:T(8,128)S(1)} %fusion.6, bf16[512,4096]{1,0:T(8,128)(2,1)S(1)} %copy-done.2, bf16[1,4096,896]{2,1,0:T(8,128)(2,1)} %bitcast), kind=kOutput, calls=%fused_computation.22 | convolution fusion | flops 1880424448 | bytes 10682368 | tf_op jit(solution)/shard_map/dot_general | solution.py:65
  165.5 0.0 copy-start.3
  165.5 0.0 copy-done
  165.5 2.8 fusion.1
  168.4 0.0 copy-done.3
  168.4 4.8 %fusion = bf16[4096,448]{0,1:T(8,128)(2,1)} fusion(bf16[512,4096]{1,0:T(8,128)(2,1)S(1)} %copy-done.2, f32[]{:T(128)} %bitcast.7, f32[512,448]{0,1:T(8,128)S(1)} %get-tuple-element.16, bf16[512,448]{0,1:T(8,128)(2,1)S(1)} %copy-done, f32[512,448]{0,1:T(8,128)S(1)} %fusion.6), kind=kOutput, calls=%fused_computation.7 | convolution fusion | flops 1883635712 | bytes 10158084 | tf_op jit(solution)/shard_map/dot_general | solution.py:85
  173.1 6.3 %pad_maximum_fusion.1 = bf16[4096,896]{0,1:T(8,128)(2,1)} fusion(bf16[4096,448]{0,1:T(8,128)(2,1)S(1)} %fusion.1, bf16[4096,448]{0,1:T(8,128)(2,1)} %fusion), kind=kLoop, calls=%fused_computation.4 | loop fusion | flops 14680064 | bytes 14680064 | tf_op jit(solution)/shard_map/concatenate | solution.py:36
  179.4 0.0 copy-start.4
  179.5 0.0 reduce-scatter.2.cloned.1.call-update
  179.5 1.2 copy-done.4
  180.6 5.0 %fusion.2 = f32[4096,512]{1,0:T(8,128)S(1)} fusion(bf16[1,4096,896]{2,1,0:T(8,128)(2,1)} %bitcast, f32[512,448]{0,1:T(8,128)S(1)} %copy-done.4, bf16[512,448]{0,1:T(8,128)(2,1)S(1)} %copy-done, f32[512,448]{0,1:T(8,128)S(1)} %fusion.6), kind=kOutput, calls=%fused_computation.11 | convolution fusion | flops 1881571328 | bytes 14876672 | tf_op jit(solution)/shard_map/dot_general | solution.py:77
  185.6 5.1 %add_convert_fusion = bf16[4096,512]{1,0:T(8,128)(2,1)S(1)} fusion(f32[4096,512]{1,0:T(8,128)S(1)} %fusion.2, bf16[1,4096,896]{2,1,0:T(8,128)(2,1)} %bitcast, bf16[512,448]{0,1:T(8,128)(2,1)S(1)} %copy-done, f32[512,448]{0,1:T(8,128)S(1)} %fusion.6), kind=kOutput, calls=%fused_computation | convolution fusion | flops 1884848128 | bytes 18153472 | tf_op jit(solution)/shard_map/dot_general | solution.py:80
  190.7 99.5 %all_to_all.17 = bf16[32,128,512]{2,1,0:T(8,128)(2,1)} all-to-all(bf16[32,128,512]{2,1,0:T(8,128)(2,1)S(1)} %bitcast.30), channel_id=1, replica_groups=mesh['pt'=8,'tp'=32] {'tp'}, dimensions={0} | all-to-all | bytes 8388608 | tf_op jit(solution)/shard_map/all_to_all | solution.py:27
  290.2 2.9 reduce_sum.12
  293.1 0.8 copy.25
  293.8 79.1 %reduce-scatter.2.cloned.1.call-done = bf16[512,896]{0,1:T(8,128)(2,1)} async-done(((bf16[4096,896]{0,1:T(8,128)(2,1)}), bf16[512,896]{0,1:T(8,128)(2,1)}) %reduce-scatter.2.cloned.1.call-update) | async-done | bytes 917520 | tf_op jit(solution)/shard_map/reduce_scatter | solution.py:38
  372.9 2.6 slice_convert_fusion
  (1 shorter events, 0.0 us)
Async XLA Ops:
  7.2 11.1 %copy-start.1 = (f32[8]{0:T(128)S(1)}, f32[8]{0:T(128)}, u32[]{:S(2)}) copy-start(f32[8]{0:T(128)} %param.10) | copy-start | bytes 100
  7.2 145.4 %all-gather.2.cloned.1.call-start = ((), (), s32[]{:S(2)}) async-start(), calls=%async_computation.3 | async-start | bytes 4325376 | tf_op jit(solution)/shard_map/all_gather | solution.py:63
  34.5 106.4 %all-to-all-start = ((bf16[8,512,896]{2,1,0:T(8,128)(2,1)}), bf16[8,512,896]{2,1,0:T(8,128)(2,1)}, u32[]{:S(2)}, u32[]{:S(2)}) async-start(bf16[8,512,896]{2,1,0:T(8,128)(2,1)} %pad_maximum_fusion), calls=%async_computation | async-start | bytes 14680064 | tf_op jit(solution)/shard_map/all_to_all | solution.py:10
  40.3 332.5 %reduce-scatter.2.cloned.1.call-start = ((), (), s32[]{:S(2)}) async-start(), calls=%async_computation.4 | async-start | bytes 8257536 | tf_op jit(solution)/shard_map/reduce_scatter | solution.py:38
  152.6 6.1 %copy-start.2 = (bf16[512,4096]{1,0:T(8,128)(2,1)S(1)}, bf16[512,4096]{1,0:T(8,128)(2,1)}, u32[]{:S(2)}) copy-start(bf16[512,4096]{1,0:T(8,128)(2,1)} %all-gather.2.cloned.1.call-done) | copy-start | bytes 12582916
  158.7 6.8 %copy-start = (bf16[512,448]{0,1:T(8,128)(2,1)S(1)}, bf16[512,448]{0,1:T(8,128)(2,1)}, u32[]{:S(2)}) copy-start(bf16[512,448]{0,1:T(8,128)(2,1)} %param.17) | copy-start | bytes 1376260
  165.5 2.8 copy-start.3
  179.4 1.2 copy-start.4
Sparse Core Ops, SparseCore 0:
  10.5 142.0 all-gather.1
  179.6 193.2 reduce-scatter.1
where the time goes:
time: 383 us; the launch traced here: 382 us
  waiting for transfers between devices  191 us (50%)
  blocking collectives  99.5 us (26%)
  matrix products  30.5 us (8%)
  other arithmetic  28.1 us (7%)
  between operations  14.1 us (4%)
  local copies, waits for them, and re-layouts  12.9 us (3%)
  starting transfers between devices  6.07 us (2%)
    all_to_all x1, waiting for transfers between devices, in_one_piece(): lax.all_to_all(both, axis, split_axis=split_dim, concat_axis=concat_dim,...  99.8 us
    all_to_all x1, blocking collectives, summed_on_arrival(): lax.all_to_all(parts, axis, split_axis=0, concat_axis=0, tiled=True)  99.5 us
    reduce_scatter x1, waiting for transfers between devices, in_one_piece_2(): lax.psum_scatter(both, axis, scatter_dimension=dim, tiled=True)  79.1 us
    all_gather x1, waiting for transfers between devices, per_device(): whole = lax.all_gather(tokens, 'tp', axis=1, tiled=True)  11.6 us
    concatenate x1, other arithmetic, in_one_piece(): both = jnp.concatenate(arrays, axis=along)  9.45 us
  transfers between devices with their start and end apart: 3, of which 3 were waited for; matrix products, arithmetic and copies ran while one was open for 11% of the time, Pallas kernels for 0%

commit v1 on v0

--- a/solution.py
+++ b/solution.py
@@ -60,7 +60,10 @@
     gate_full, up_full = in_one_piece((gate_parts, up_parts), "pt", 0, 1, 2)
     gate_w = gate_full[0]
     up_w = up_full[0]
-    whole = lax.all_gather(tokens, "tp", axis=1, tiled=True)
+    devices = lax.axis_size("tp")
+    tiles = jnp.stack([tokens for _ in range(devices)])
+    tiles = lax.all_to_all(tiles, "tp", split_axis=0, concat_axis=0)
+    whole = jnp.concatenate(tiles, axis=1)
     gate = jnp.dot(whole, gate_w, preferred_element_type=jnp.float32)
     up = jnp.dot(whole, up_w, preferred_element_type=jnp.float32)
     sig = jax.nn.sigmoid(gate)

time: 383 us -> 488 us (1.27)
  waiting for transfers between devices: 191 us -> 273 us
  starting transfers between devices: 6.07 us -> 19.4 us
    all_to_all x0 -> x1, waiting for transfers between devices: none -> 95.4 us  [per_device(): tiles = lax.all_to_all(tiles, 'tp', split_axis=0, concat_axis=0)]
    all_to_all x0 -> x1, starting transfers between devices: none -> 13.2 us  [per_device(): tiles = lax.all_to_all(tiles, 'tp', split_axis=0, concat_axis=0)]
    all_gather x1 -> x0, waiting for transfers between devices: 11.6 us -> none  [per_device(): whole = lax.all_gather(tokens, 'tp', axis=1, tiled=True)]
  transfers between devices with their start and end apart: 3 -> 3, of which waited for: 3 -> 3; matrix products, arithmetic and copies ran while one was open for 11% -> 3% of each run, Pallas kernels for 0% -> 0%
where the time goes in v1:
time: 488 us; the launch traced here: 487 us
  waiting for transfers between devices  273 us (56%)
  blocking collectives  102 us (21%)
  matrix products  34.4 us (7%)
  other arithmetic  28.7 us (6%)
  starting transfers between devices  19.4 us (4%)
  local copies, waits for them, and re-layouts  15.5 us (3%)
  between operations  14.1 us (3%)
    all_to_all x1, blocking collectives, summed_on_arrival(): lax.all_to_all(parts, axis, split_axis=0, concat_axis=0, tiled=True)  102 us
    all_to_all x1, waiting for transfers between devices, in_one_piece(): lax.all_to_all(both, axis, split_axis=split_dim, concat_axis=concat_dim,...  100 us
    all_to_all x1, waiting for transfers between devices, per_device(): tiles = lax.all_to_all(tiles, 'tp', split_axis=0, concat_axis=0)  95.4 us
    reduce_scatter x1, waiting for transfers between devices, in_one_piece_2(): lax.psum_scatter(both, axis, scatter_dimension=dim, tiled=True)  77 us
    all_to_all x1, starting transfers between devices, per_device(): tiles = lax.all_to_all(tiles, 'tp', split_axis=0, concat_axis=0)  13.2 us
  transfers between devices with their start and end apart: 3, of which 3 were waited for; matrix products, arithmetic and copies ran while one was open for 3% of the time, Pallas kernels for 0%

profile of v1, /device:TPU:1, one launch (start us, length us, event | category | flops | bytes accessed | tf_op | source)
XLA Modules:
  0.0 487.2 jit_solution(2278433525755471577)
XLA Ops:
  7.2 0.7 subtract_multiply_fusion
  7.8 1.2 copy.26
  9.1 1.2 copy.27
  10.3 1.2 copy.28
  11.5 2.2 copy.29
  13.7 2.2 copy.30
  15.9 2.3 copy.31
  18.2 6.8 %add_convert_fusion.2 = (bf16[8,512,448]{2,1,0:T(8,128)(2,1)}, bf16[8,512,448]{2,1,0:T(8,128)(2,1)}) fusion(f32[512,448]{1,0:T(8,128)S(1)} %copy.28, f32[8]{0:T(128)S(1)} %get-tuple-element.13, f32[512,448]{1,0:T(8,128)S(1)} %copy.27, f32[8]{0:T(128)S(1)} %get-tuple-element.14, f32[512,448]{1,0:T(8,128)S(1)} %copy.26, f32[8]{0:T(128)S(1)} %get-tuple-element.12, ...), kind=kLoop, calls=%fused_computation.2 | loop fusion | flops 22020096 | bytes 12845152 | tf_op jit(solution)/shard_map/convert_element_type | solution.py:48
  25.0 9.4 %pad_maximum_fusion = bf16[8,512,896]{2,1,0:T(8,128)(2,1)} fusion(bf16[8,512,448]{2,1,0:T(8,128)(2,1)} %get-tuple-element.11, bf16[8,512,448]{2,1,0:T(8,128)(2,1)} %get-tuple-element.10), kind=kLoop, calls=%fused_computation.3 | loop fusion | flops 14680064 | bytes 14680064 | tf_op jit(solution)/shard_map/concatenate | solution.py:8
  34.4 0.0 copy-start.1
  34.4 6.0 %all-to-all-start = ((bf16[8,512,896]{2,1,0:T(8,128)(2,1)}), bf16[8,512,896]{2,1,0:T(8,128)(2,1)}, u32[]{:S(2)}, u32[]{:S(2)}) async-start(bf16[8,512,896]{2,1,0:T(8,128)(2,1)} %pad_maximum_fusion), calls=%async_computation | async-start | bytes 14680064 | tf_op jit(solution)/shard_map/all_to_all | solution.py:10
  40.4 0.0 copy-done.1
  40.4 0.1 copy.32
  40.5 100.4 %all-to-all-done = bf16[8,512,896]{2,1,0:T(8,128)(2,1)} async-done(((bf16[8,512,896]{2,1,0:T(8,128)(2,1)}), bf16[8,512,896]{2,1,0:T(8,128)(2,1)}, u32[]{:S(2)}, u32[]{:S(2)}) %all-to-all-start) | async-done | bytes 7340064 | tf_op jit(solution)/shard_map/all_to_all | solution.py:10
  140.9 2.5 stack.2
  143.4 13.2 %all-to-all-start.1 = ((bf16[32,512,128]{1,2,0:T(8,128)(2,1)}), bf16[32,512,128]{1,2,0:T(8,128)(2,1)}, u32[]{:S(2)}, u32[]{:S(2)}) async-start(bf16[32,512,128]{1,2,0:T(8,128)(2,1)} %stack.2), calls=%async_computation.1 | async-start | bytes 8388608 | tf_op jit(solution)/shard_map/all_to_all | solution.py:65
  156.6 0.2 reduce-scatter.2.cloned.1.call-start
  156.8 0.6 dynamic_slice.4
  157.4 95.4 %all-to-all-done.1 = bf16[32,512,128]{1,2,0:T(8,128)(2,1)} async-done(((bf16[32,512,128]{1,2,0:T(8,128)(2,1)}), bf16[32,512,128]{1,2,0:T(8,128)(2,1)}, u32[]{:S(2)}, u32[]{:S(2)}) %all-to-all-start.1) | async-done | bytes 4194336 | tf_op jit(solution)/shard_map/all_to_all | solution.py:65
  252.8 5.5 %fusion.6 = f32[512,448]{0,1:T(8,128)S(1)} fusion(bf16[512,4096]{0,1:T(8,128)(2,1)} %bitcast.3, bf16[1,4096,896]{2,1,0:T(8,128)(2,1)} %bitcast), kind=kOutput, calls=%fused_computation.15 | convolution fusion | flops 1879048192 | bytes 9306112 | tf_op jit(solution)/shard_map/dot_general | solution.py:67
  258.4 0.0 copy-start
  258.4 7.3 %multiply_convert_fusion.2 = (bf16[512,448]{0,1:T(8,128)(2,1)}, f32[512,448]{0,1:T(8,128)S(1)}) fusion(f32[512,448]{0,1:T(8,128)S(1)} %fusion.6, bf16[512,4096]{0,1:T(8,128)(2,1)} %bitcast.3, bf16[1,4096,896]{2,1,0:T(8,128)(2,1)} %bitcast), kind=kOutput, calls=%fused_computation.22 | convolution fusion | flops 1880424448 | bytes 10682368 | tf_op jit(solution)/shard_map/dot_general | solution.py:68
  265.6 0.0 copy-start.2
  265.6 0.0 copy-done
  265.6 5.0 %fusion.1 = bf16[4096,448]{0,1:T(8,128)(2,1)S(1)} fusion(bf16[512,4096]{0,1:T(8,128)(2,1)} %bitcast.3, bf16[512,448]{0,1:T(8,128)(2,1)S(1)} %copy-done, f32[]{:T(128)} %bitcast.10, f32[512,448]{0,1:T(8,128)S(1)} %fusion.6), kind=kOutput, calls=%fused_computation.8 | convolution fusion | flops 1882718208 | bytes 9240580 | tf_op jit(solution)/shard_map/dot_general | solution.py:91
  270.6 0.0 copy-done.2
  270.6 6.9 %fusion = bf16[4096,448]{0,1:T(8,128)(2,1)} fusion(bf16[512,4096]{0,1:T(8,128)(2,1)} %bitcast.3, f32[]{:T(128)} %bitcast.10, f32[512,448]{0,1:T(8,128)S(1)} %get-tuple-element.16, bf16[512,448]{0,1:T(8,128)(2,1)S(1)} %copy-done, f32[512,448]{0,1:T(8,128)S(1)} %fusion.6), kind=kOutput, calls=%fused_computation.7 | convolution fusion | flops 1883635712 | bytes 10158084 | tf_op jit(solution)/shard_map/dot_general | solution.py:88
  277.5 6.3 %pad_maximum_fusion.1 = bf16[4096,896]{0,1:T(8,128)(2,1)} fusion(bf16[4096,448]{0,1:T(8,128)(2,1)S(1)} %fusion.1, bf16[4096,448]{0,1:T(8,128)(2,1)} %fusion), kind=kLoop, calls=%fused_computation.4 | loop fusion | flops 14680064 | bytes 14680064 | tf_op jit(solution)/shard_map/concatenate | solution.py:36
  283.9 0.0 copy-start.3
  283.9 0.0 reduce-scatter.2.cloned.1.call-update
  283.9 1.2 copy-done.3
  285.0 4.7 fusion.2
  289.8 5.0 %add_convert_fusion = bf16[4096,512]{1,0:T(8,128)(2,1)S(1)} fusion(f32[4096,512]{1,0:T(8,128)S(1)} %fusion.2, bf16[1,4096,896]{2,1,0:T(8,128)(2,1)} %bitcast, bf16[512,448]{0,1:T(8,128)(2,1)S(1)} %copy-done, f32[512,448]{0,1:T(8,128)S(1)} %fusion.6), kind=kOutput, calls=%fused_computation | convolution fusion | flops 1884848128 | bytes 18153472 | tf_op jit(solution)/shard_map/dot_general | solution.py:83
  294.8 102.4 %all_to_all.22 = bf16[32,128,512]{2,1,0:T(8,128)(2,1)} all-to-all(bf16[32,128,512]{2,1,0:T(8,128)(2,1)S(1)} %bitcast.33), channel_id=1, replica_groups=mesh['pt'=8,'tp'=32] {'tp'}, dimensions={0} | all-to-all | bytes 8388608 | tf_op jit(solution)/shard_map/all_to_all | solution.py:27
  397.2 2.8 reduce_sum.12
  400.0 0.8 copy.33
  400.8 77.0 %reduce-scatter.2.cloned.1.call-done = bf16[512,896]{0,1:T(8,128)(2,1)} async-done(((bf16[4096,896]{0,1:T(8,128)(2,1)}), bf16[512,896]{0,1:T(8,128)(2,1)}) %reduce-scatter.2.cloned.1.call-update) | async-done | bytes 917520 | tf_op jit(solution)/shard_map/reduce_scatter | solution.py:38
  477.7 2.6 slice_convert_fusion
Async XLA Ops:
  34.4 6.0 %copy-start.1 = (bf16[512,128]{1,0:T(8,128)(2,1)S(1)}, bf16[512,128]{1,0:T(8,128)(2,1)}, u32[]{:S(2)}) copy-start(bf16[512,128]{1,0:T(8,128)(2,1)} %param.9) | copy-start | bytes 393220
  34.4 106.5 %all-to-all-start = ((bf16[8,512,896]{2,1,0:T(8,128)(2,1)}), bf16[8,512,896]{2,1,0:T(8,128)(2,1)}, u32[]{:S(2)}, u32[]{:S(2)}) async-start(bf16[8,512,896]{2,1,0:T(8,128)(2,1)} %pad_maximum_fusion), calls=%async_computation | async-start | bytes 14680064 | tf_op jit(solution)/shard_map/all_to_all | solution.py:10
  143.4 109.4 %all-to-all-start.1 = ((bf16[32,512,128]{1,2,0:T(8,128)(2,1)}), bf16[32,512,128]{1,2,0:T(8,128)(2,1)}, u32[]{:S(2)}, u32[]{:S(2)}) async-start(bf16[32,512,128]{1,2,0:T(8,128)(2,1)} %stack.2), calls=%async_computation.1 | async-start | bytes 8388608 | tf_op jit(solution)/shard_map/all_to_all | solution.py:65
  156.6 321.1 %reduce-scatter.2.cloned.1.call-start = ((), (), s32[]{:S(2)}) async-start(), calls=%async_computation.4 | async-start | bytes 8257536 | tf_op jit(solution)/shard_map/reduce_scatter | solution.py:38
  258.4 7.3 %copy-start = (bf16[512,448]{0,1:T(8,128)(2,1)S(1)}, bf16[512,448]{0,1:T(8,128)(2,1)}, u32[]{:S(2)}) copy-start(bf16[512,448]{0,1:T(8,128)(2,1)} %param.17) | copy-start | bytes 1376260
  265.6 5.0 %copy-start.2 = (f32[512,448]{0,1:T(8,128)}, f32[512,448]{0,1:T(8,128)S(1)}, u32[]{:S(2)}) copy-start(f32[512,448]{0,1:T(8,128)S(1)} %get-tuple-element.16) | copy-start | bytes 2752516
  283.9 1.2 copy-start.3
Sparse Core Ops, SparseCore 0:
  284.0 193.6 reduce-scatter.1
